TPU v7x, 512 devices: a whole 4x4x16 slice. The times are simulated.
512 devices in a mesh: leaf: 128 (over z, x, core), lvl: 4 (over y).
Axes of the slice: x: 4, y: 4, z: 16, core: 2. Of those that a mesh axis runs over, the one named last changes fastest.
Arguments:
- offsets: float32 [3, 262144], P(None, 'leaf'), may hold values from -0.5 to 0.5
- vel_cot: float32 [3, 262144], P(None, 'leaf'), may hold values from -0.18 to 0.18
- m2l_ops: bfloat16 [16, 456, 456], P('lvl'), may hold values from -0.25 to 0.25
- child_ops: bfloat16 [8, 456, 456], P('lvl'), may hold values from -0.25 to 0.25
- check_map: float32 [456, 456], replicated, may hold values from -0.015625 to 0.015625
- leaf_dest: int32 [4, 4096, 4, 1], P('lvl', 'leaf'), may hold values from 0 to 127; in each aligned block of 128 rows (0 to 127, 128 to 255, ..., all dimensions but the last counted through in order) at most 2 rows name the same one
- leaf_slot: int32 [4, 4096, 4], P('lvl', 'leaf'), may hold values from 0 to 31
- coarse_dest: int32 [4, 512, 4, 1], P('lvl'), may hold values from 0 to 127
- coarse_slot: int32 [4, 512, 4], P('lvl'), may hold values from 0 to 3
- near_box: int32 [4096, 16], P('leaf', 'lvl'), may hold values from 0 to 31
- near_dir: int32 [4096, 16], P('leaf', 'lvl'), may hold values from 0 to 26
Outputs:
- force_cot: float32 [3, 262144], P(None, 'leaf')
Inputs may be any that keep to these rules, and one draw needn't show every extreme that they name: `leaf_dest`: in the rows of one device (aligned blocks of 128 rows in the order of the leading dimensions) no subtree is named more than 2 times. `near_box`: A place among the 32 leaf boxes of the same subtree.
All inputs are finite; a program needn't handle non-finite values.
Results may differ from a plain program's by a relative error of at most 0.0095.
Values may be sent and summed in bfloat16 or wider, within the bound.
A program may use at most 64 MiB of HBM per device.

v0:
```python
import jax
import jax.numpy as jnp
import numpy as np
from jax import lax
from jax.sharding import Mesh
from jax.sharding import PartitionSpec as P

SIDE = 6
LEAF = ("leaf_0", "leaf_1", "leaf_2")


EPSILON2 = 0.01
RADIUS = 0.525


def sent_to_all(value, axis):
    peers = lax.axis_size(axis)
    return lax.all_to_all(
        jnp.broadcast_to(value[None], (peers, *value.shape)), axis, 0, 0, tiled=True
    )


def taken_together(value, axis):
    everything = sent_to_all(value, axis)
    return jnp.sum(everything, axis=0)


def joined_along(tiles, dim):
    tiles = jnp.moveaxis(tiles, 0, dim)
    shape = tiles.shape
    return tiles.reshape(*shape[:dim], shape[dim] * shape[dim + 1], *shape[dim + 2 :])


def all_blocks(value, axes, turns):
    tiles = value
    for k in turns:
        tiles = lax.all_gather(tiles, axes[k])
    done = turns[::-1]
    back = [done.index(k) for k in range(len(axes))]
    tiles = tiles.transpose(*back, *range(len(axes), tiles.ndim))
    return tiles.reshape(-1, *value.shape)


def whole_of(value, axes, turns, dim):
    return joined_along(all_blocks(value, axes, turns), dim)


def surface_points(edge_count):
    levels = np.linspace(-1.0, 1.0, edge_count)
    lattice = np.stack(np.meshgrid(levels, levels, levels, indexing="ij"), 0).reshape(3, -1)
    on_shell = np.max(np.abs(lattice), 0) > 1.0 - 1e-09
    return jnp.asarray(lattice[:, on_shell] * RADIUS, jnp.float32)


def stokes_apply(relative, source):
    squared = jnp.sum(relative * relative, axis=0)
    weights = (squared + EPSILON2) ** (-1.5)
    spread = source[..., None, :]
    along = jnp.sum(relative * spread, axis=0)
    return jnp.sum(weights * ((squared + 2.0 * EPSILON2) * spread + relative * along), axis=-1)


def to_surface(points, vectors, shell):
    relative = shell[:, None, :, None] - points[:, :, None, :]
    values = stokes_apply(relative, vectors)
    return values.transpose(1, 0, 2).reshape(values.shape[1], -1)


def from_surface(points, density, shell):
    source = density.reshape(density.shape[0], 3, -1).transpose(1, 0, 2)
    relative = points[:, :, :, None] - shell[:, None, None, :]
    return stokes_apply(relative, source)


def directions(codes):
    return jnp.stack([codes // 9 - 1, codes // 3 % 3 - 1, codes % 3 - 1], 0).astype(jnp.float32)


def near_terms(points, src_points, src_vectors, shifts):
    moved = src_points + shifts[..., None]
    relative = points[:, :, None, :, None] - moved[:, :, :, None, :]
    return jnp.sum(stokes_apply(relative, src_vectors), axis=2)


def local(
    offsets,
    vel_cot,
    m2l_ops,
    child_ops,
    check_map,
    leaf_dest,
    leaf_slot,
    coarse_dest,
    coarse_slot,
    near_box,
    near_dir,
):
    shell = surface_points(SIDE)
    width = m2l_ops.shape[1]
    classes_here = m2l_ops.shape[0]
    octants_here = child_ops.shape[0]
    boxes = near_box.shape[0]
    per_box = offsets.shape[1] // boxes
    parents = boxes // 8
    blocks = boxes // 8
    items = boxes * classes_here
    leaf_count = lax.axis_size(LEAF)
    capacity = max(2, (2 * items + leaf_count - 1) // leaf_count)
    leaf_index = lax.axis_index(LEAF)
    lvl_index = lax.axis_index("lvl")
    points = offsets.reshape(3, boxes, per_box)
    vectors = vel_cot.reshape(3, boxes, per_box)
    point_blocks = points.reshape(3, blocks, 8, per_box).transpose(1, 0, 2, 3)
    vector_blocks = vectors.reshape(3, blocks, 8, per_box).transpose(1, 0, 2, 3)
    local_float = lax.map(
        lambda packed: to_surface(packed[0], packed[1], shell), (point_blocks, vector_blocks)
    )
    leaf_local = local_float.reshape(boxes, width).astype(jnp.bfloat16)
    leaf_terms = jnp.einsum("tm,cmn->tcn", leaf_local, m2l_ops, preferred_element_type=jnp.float32)
    leaf_terms = leaf_terms.astype(jnp.bfloat16).reshape(items, width)
    owners = leaf_dest[0, :, :, 0].reshape(items)
    places = leaf_slot[0].reshape(items)
    owner_hits = (owners[:, None] == jnp.arange(leaf_count, dtype=jnp.int32)[None, :]).astype(
        jnp.int32
    )
    earlier = jnp.cumsum(owner_hits, axis=0) - owner_hits
    send_pos = owners * capacity + jnp.sum(earlier * owner_hits, axis=1)
    placing = send_pos[None, :] == jnp.arange(leaf_count * capacity, dtype=jnp.int32)[:, None]
    send_rows = jnp.dot(
        placing.astype(jnp.bfloat16), leaf_terms, preferred_element_type=jnp.float32
    ).astype(jnp.bfloat16)
    send_ids = jnp.dot(
        placing.astype(jnp.float32),
        (places + 1).astype(jnp.float32),
        precision=lax.Precision.HIGHEST,
    )
    send_ids = send_ids.astype(jnp.int32) - 1
    got_rows, got_ids = (
        lax.all_to_all(
            send_rows.reshape(leaf_count, capacity, width),
            LEAF,
            split_axis=0,
            concat_axis=0,
            tiled=True,
        ),
        lax.all_to_all(
            send_ids.reshape(leaf_count, capacity), LEAF, split_axis=0, concat_axis=0, tiled=True
        ),
    )
    landing = got_ids.reshape(-1)[None, :] == jnp.arange(boxes, dtype=jnp.int32)[:, None]
    leaf_far = jnp.dot(
        landing.astype(jnp.bfloat16),
        got_rows.reshape(-1, width),
        preferred_element_type=jnp.float32,
    )
    children = leaf_local.reshape(parents, 8, width)
    my_children = lax.dynamic_slice_in_dim(children, lvl_index * octants_here, octants_here, 1)
    parent_part = jnp.einsum(
        "pom,omn->pn", my_children, child_ops, preferred_element_type=jnp.float32
    )
    parent_local = taken_together(parent_part, "lvl").astype(jnp.bfloat16)
    coarse_ids = coarse_dest[0, :, :, 0] * parents + coarse_slot[0]
    mine = leaf_index * parents + jnp.arange(parents, dtype=jnp.int32)
    terms = 0.5 * jnp.einsum(
        "rm,cmn->crn",
        whole_of(parent_local, LEAF, (1, 0, 2), 0),
        m2l_ops,
        preferred_element_type=jnp.float32,
    )
    select = (coarse_ids.T[:, None, :] == mine[None, :, None]).astype(jnp.float32)
    coarse_part = jnp.einsum("cpr,crn->pn", select, terms, precision=lax.Precision.HIGHEST)
    parent_mult = taken_together(coarse_part, "lvl").astype(jnp.bfloat16)
    lowered = jnp.einsum("pm,onm->pon", parent_mult, child_ops, preferred_element_type=jnp.float32)
    placed = lax.dynamic_update_slice_in_dim(
        jnp.zeros((parents, 8, width), jnp.float32), lowered, lvl_index * octants_here, 1
    )
    leaf_part = leaf_far + placed.reshape(boxes, width)
    neighbour_blocks = near_box.reshape(blocks, 8, near_box.shape[1])
    shift_blocks = (
        directions(near_dir).reshape(3, blocks, 8, near_box.shape[1]).transpose(1, 0, 2, 3)
    )

    def near_block(packed):
        here, chosen, moved = packed
        return near_terms(here, points[:, chosen], vectors[:, chosen], moved)

    near_blocks = lax.map(near_block, (point_blocks, neighbour_blocks, shift_blocks))
    near_part = near_blocks.transpose(1, 0, 2, 3).reshape(3, boxes * per_box)
    check_part = jnp.dot(leaf_part, check_map, precision=lax.Precision.HIGHEST)
    check_blocks = check_part.reshape(blocks, 8, width)
    far_blocks = lax.map(
        lambda packed: from_surface(packed[0], packed[1], shell), (point_blocks, check_blocks)
    )
    return taken_together(
        far_blocks.transpose(1, 0, 2, 3).reshape(3, boxes * per_box) + near_part, "lvl"
    )


def solution(mesh):
    torus = Mesh(
        mesh.devices.reshape(16, 4, 2, mesh.shape["lvl"]), ("leaf_0", "leaf_1", "leaf_2", "lvl")
    )
    in_specs = (
        P(None, LEAF),
        P(None, LEAF),
        P("lvl", None, None),
        P("lvl", None, None),
        P(),
        P("lvl", LEAF, None, None),
        P("lvl", LEAF, None),
        P("lvl", None, None, None),
        P("lvl", None, None),
        P(LEAF, "lvl"),
        P(LEAF, "lvl"),
    )
    out_specs = P(None, LEAF)
    return jax.shard_map(local, mesh=torus, in_specs=in_specs, out_specs=out_specs, check_vma=False)
```

profile of v0, /device:TPU:1, one launch (start us, length us, event | category | flops | bytes accessed | tf_op | source)
XLA Modules:
  0.0 154.7 jit_solution(107992814119449124)
XLA Ops:
  0.0 1.0 reshape_reshape.9
  1.0 0.9 reshape_reshape.10
  1.9 9.3 %while.33 = (s32[]{:T(128)}, bf16[4,8,456]{2,0,1:T(4,128)(2,1)S(1)}, f32[4,3,8,64]{3,2,1,0:T(8,128)S(1)}, f32[4,3,8,64]{3,2,0,1:T(8,128)S(1)}, s32[]{:T(128)}, /*index=5*/f32[3,152]{1,0:T(4,128)}, s32[]{:T(128)}) while((s32[]{:T(128)}, bf16[4,8,456]{2,0,1:T(4,128)(2,1)S(1)}, f32[4,3,8,64]{3,2,1,0:T(8,128)S(1)}, ...), condition=%wide.region_6.7_spmd.clone, body=%wide.region_2.6_spmd.sunk.clone.sunk | while | flops 2564546 | bytes 2601653 | solution.py:115
  1.9 1.3 fusion.64
  3.5 0.6 fusion.65
  4.3 1.2 fusion.64
  5.8 0.6 fusion.65
  6.6 1.2 fusion.64
  8.1 0.6 fusion.65
  8.9 1.2 fusion.64
  10.4 0.6 fusion.65
  11.5 0.6 broadcast_in_dim.22
  12.1 5.0 %all-to-all-start.2 = ((f32[4,4,456]{2,1,0:T(4,128)}), f32[4,4,456]{2,1,0:T(4,128)S(1)}, u32[]{:S(2)}, u32[]{:S(2)}) async-start(f32[4,4,456]{2,1,0:T(4,128)} %broadcast_in_dim.22), calls=%async_computation.2 | async-start | bytes 65536 | tf_op jit(solution)/shard_map/all_to_all | solution.py:18
  17.8 0.4 convolution_convert_fusion.1
  18.6 1.0 convolution_convert_fusion
  19.9 0.8 all_to_all.18
  20.9 0.5 all-to-all-done.2
  21.4 21.0 %all-to-all-start = ((s32[128,1,2]{2,1,0:T(1,128)}), s32[128,1,2]{2,1,0:T(1,128)S(1)}, u32[]{:S(2)}, u32[]{:S(2)}) async-start(s32[128,1,2]{2,1,0:T(1,128)} %bitcast.10), calls=%async_computation | async-start | bytes 131072 | tf_op jit(solution)/shard_map/all_to_all | solution.py:146
  42.4 9.6 %all-gather.3 = bf16[4,4,456]{2,1,0:T(4,128)(2,1)S(1)} all-gather(bf16[1,4,456]{2,1,0:T(4,128)(2,1)S(1)} %bitcast.134), channel_id=2, replica_groups=mesh['leaf_0'=16,'leaf_1'=4,'leaf_2'=2,'lvl'=4] {'leaf_1'}, dimensions={0}, use_global_device_ids=true | all-gather | bytes 18240 | tf_op jit(solution)/shard_map/all_gather | solution.py:37
  52.0 24.3 %all-gather.1 = bf16[64,4,456]{2,1,0:T(4,128)(2,1)S(1)} all-gather(bf16[4,4,456]{2,1,0:T(4,128)(2,1)S(1)} %all-gather.3), channel_id=3, replica_groups=mesh['leaf_0'=16,'leaf_1'=4,'leaf_2'=2,'lvl'=4] {'leaf_0'}, dimensions={0}, use_global_device_ids=true | all-gather | bytes 248064 | tf_op jit(solution)/shard_map/all_gather | solution.py:37
  76.3 12.0 %all-gather.2 = bf16[32,4,4,456]{3,2,1,0:T(4,128)(2,1)S(1)} all-gather(bf16[16,4,4,456]{3,2,1,0:T(4,128)(2,1)S(1)} %bitcast.129), channel_id=4, replica_groups=mesh['leaf_0'=16,'leaf_1'=4,'leaf_2'=2,'lvl'=4] {'leaf_2'}, dimensions={0}, use_global_device_ids=true | all-gather | bytes 700416 | tf_op jit(solution)/shard_map/all_gather | solution.py:37
  88.6 1.2 copy.165
  89.8 1.3 reshape_reshape.11
  91.1 1.2 fusion.22
  92.3 1.9 %fusion.19 = f32[4,456]{1,0:T(4,128)S(1)} fusion(f32[512,4,456]{0,2,1:T(8,128)S(1)} %fusion.22, s32[4,512]{1,0:T(4,128)S(1)} %fusion.35, s32[4]{0:T(128)S(1)} %iota_add_fusion), kind=kOutput, calls=%fused_computation.52 | convolution fusion | flops 45768704 | bytes 3751056 | tf_op jit(solution)/shard_map/cpr,crn->pn/dot_general | solution.py:171
  94.2 0.6 broadcast_in_dim.23
  94.8 3.9 %all-to-all-start.3 = ((f32[4,4,456]{2,1,0:T(4,128)}), f32[4,4,456]{2,1,0:T(4,128)}, u32[]{:S(2)}, u32[]{:S(2)}) async-start(f32[4,4,456]{2,1,0:T(4,128)} %broadcast_in_dim.23), calls=%async_computation.3 | async-start | bytes 65536 | tf_op jit(solution)/shard_map/all_to_all | solution.py:18
  98.7 0.6 fusion.31
  99.7 0.8 reshape.157
  100.6 2.4 %all-to-all-done.3 = f32[4,4,456]{2,1,0:T(4,128)} async-done(((f32[4,4,456]{2,1,0:T(4,128)}), f32[4,4,456]{2,1,0:T(4,128)}, u32[]{:S(2)}, u32[]{:S(2)}) %all-to-all-start.3) | async-done | bytes 29216 | tf_op jit(solution)/shard_map/all_to_all | solution.py:18
  103.1 13.3 %all-to-all-start.1 = ((bf16[128,2,456]{2,1,0:T(2,128)(2,1)}), bf16[128,2,456]{2,1,0:T(2,128)(2,1)S(1)}, u32[]{:S(2)}, u32[]{:S(2)}) async-start(bf16[128,2,456]{2,1,0:T(2,128)(2,1)} %reshape.157), calls=%async_computation.1 | async-start | bytes 524288 | tf_op jit(solution)/shard_map/all_to_all | solution.py:139
  116.4 19.3 %while.32 = (s32[]{:T(128)}, f32[4,3,8,64]{3,2,1,0:T(8,128)S(1)}, f32[4,3,8,64]{3,2,1,0:T(8,128)S(1)}, s32[4,8,4]{1,0,2:T(4,128)S(1)}, f32[3,32,64]{2,0,1:T(4,12...) while((s32[]{:T(128)}, f32[4,3,8,64]{3,2,1,0:T(8,128)S(1)}, ...), condition=%wide.region_18.19_spmd, body=%wide.region_14.18_spmd.sunk | while | flops 4331106 | bytes 4601189 | solution.py:187
  116.6 0.6 gather_fusion
  117.2 0.8 constant_dynamic-slice_fusion.7
  118.2 0.6 gather_fusion.1
  118.8 0.8 fusion.62
  119.6 0.4 add_power_fusion.6
  120.0 1.2 fusion.63
  121.4 0.6 gather_fusion
  122.0 0.8 constant_dynamic-slice_fusion.7
  123.0 0.6 gather_fusion.1
  123.6 0.8 fusion.62
  124.8 1.2 fusion.63
  126.2 0.6 gather_fusion
  126.8 0.8 constant_dynamic-slice_fusion.7
  127.8 0.6 gather_fusion.1
  128.5 0.8 fusion.62
  129.6 1.2 fusion.63
  131.0 0.6 gather_fusion
  131.6 0.8 constant_dynamic-slice_fusion.7
  132.6 0.6 gather_fusion.1
  133.3 0.8 fusion.62
  134.5 1.2 fusion.63
  135.6 0.5 broadcast.180
  136.2 0.8 reduce.4
  137.1 0.8 reduce_sum.123
  138.7 1.8 %convolution_bitcast_fusion = f32[4,8,456]{2,1,0:T(8,128)S(1)} fusion(f32[32,456]{1,0:T(8,128)S(1)} %convolution_add_fusion, f32[456,456]{1,0:T(8,128)} %param.22), kind=kOutput, calls=%fused_computation.50 | convolution fusion | flops 79847424 | bytes 948480 | tf_op jit(solution)/shard_map/dot_general | solution.py:189
  140.5 6.1 %while.34 = (s32[]{:T(128)}, f32[4,3,8,64]{3,2,1,0:T(8,128)S(1)}, f32[4,3,8,64]{3,2,1,0:T(8,128)S(1)}, f32[4,8,456]{2,1,0:T(8,128)S(1)}, s32[]{:T(128)}, /*index=5*/f32[3,152]{1,0:T(4,128)S(1)}) while((s32[]{:T(128)}, f32[4,3,8,64]{3,2,1,0:T(8,128)S(1)}, f32[4,3,8,64]{3,2,1,0:T(8,128)S(1)}, f32[4,8,456]{2,1,0:T(8,128)S(1)}, ...), condition=%wide.region_13.14_spmd.clone, body=%wide.region_9.13_spmd.sunk.clone.sunk | while | flops 2566658 | bytes 2666129 | solution.py:191
  141.3 0.8 fusion.67
  142.8 0.8 fusion.67
  144.3 0.8 fusion.67
  145.9 0.8 fusion.67
  146.8 7.2 %all_to_all.29 = f32[4,3,2048]{2,1,0:T(4,128)S(1)} all-to-all(f32[4,3,2048]{2,1,0:T(4,128)S(1)} %broadcast_in_dim.24), channel_id=1, replica_groups=mesh['leaf_0'=16,'leaf_1'=4,'leaf_2'=2,'lvl'=4] {'lvl'}, dimensions={0} | all-to-all | bytes 196608 | tf_op jit(solution)/shard_map/all_to_all | solution.py:18
  154.0 0.6 reduce_sum.124
  (175 shorter events, 11.0 us)
Async XLA Ops:
  0.0 17.8 %copy-start = (bf16[4,456,456]{2,1,0:T(8,128)(2,1)S(1)}, bf16[4,456,456]{2,1,0:T(8,128)(2,1)}, u32[]{:S(2)}) copy-start(bf16[4,456,456]{2,1,0:T(8,128)(2,1)} %param.20) | copy-start | bytes 4990468
  1.9 9.3 %copy-start.1 = (bf16[2,456,456]{2,1,0:T(8,128)(2,1)S(1)}, bf16[2,456,456]{2,1,0:T(8,128)(2,1)}, u32[]{:S(2)}) copy-start(bf16[2,456,456]{2,1,0:T(8,128)(2,1)} %param.21) | copy-start | bytes 2495236
  1.9 15.2 %copy-start.9 = (s32[1,32,4,1]{1,3,2,0:T(1,128)S(1)}, s32[1,32,4,1]{1,3,2,0:T(1,128)}, u32[]{:S(2)}) copy-start(s32[1,32,4,1]{1,3,2,0:T(1,128)} %param.23) | copy-start | bytes 1540
  1.9 1.6 %copy-start.4 = (f32[3,152]{1,0:T(4,128)S(1)}, f32[3,152]{1,0:T(4,128)}, u32[]{:S(2)}) copy-start(f32[3,152]{1,0:T(4,128)} %get-tuple-element.407) | copy-start | bytes 5476 | tf_op jit(solution)/shard_map/while
  4.3 1.5 copy-start.4
  6.6 1.5 copy-start.4
  8.9 1.5 copy-start.4
  11.4 6.9 %copy-start.11 = (s32[1,32,4]{1,2,0:T(4,128)S(1)}, s32[1,32,4]{1,2,0:T(4,128)}, u32[]{:S(2)}) copy-start(s32[1,32,4]{1,2,0:T(4,128)} %param.24) | copy-start | bytes 1540
  12.1 9.3 %all-to-all-start.2 = ((f32[4,4,456]{2,1,0:T(4,128)}), f32[4,4,456]{2,1,0:T(4,128)S(1)}, u32[]{:S(2)}, u32[]{:S(2)}) async-start(f32[4,4,456]{2,1,0:T(4,128)} %broadcast_in_dim.22), calls=%async_computation.2 | async-start | bytes 65536 | tf_op jit(solution)/shard_map/all_to_all | solution.py:18
  17.4 2.4 %copy-start.12 = (s32[32,4]{0,1:T(4,128)S(1)}, s32[32,4]{0,1:T(4,128)}, u32[]{:S(2)}) copy-start(s32[32,4]{0,1:T(4,128)} %param.28) | copy-start | bytes 1540
  17.4 2.4 %copy-start.7 = (s32[1,512,4]{1,2,0:T(4,128)S(1)}, s32[1,512,4]{1,2,0:T(4,128)}, u32[]{:S(2)}) copy-start(s32[1,512,4]{1,2,0:T(4,128)} %param.26) | copy-start | bytes 24580
  17.4 2.4 %copy-start.8 = (s32[1,512,4,1]{1,3,2,0:T(1,128)S(1)}, s32[1,512,4,1]{1,3,2,0:T(1,128)}, u32[]{:S(2)}) copy-start(s32[1,512,4,1]{1,3,2,0:T(1,128)} %param.25) | copy-start | bytes 24580
  21.4 72.8 %all-to-all-start = ((s32[128,1,2]{2,1,0:T(1,128)}), s32[128,1,2]{2,1,0:T(1,128)S(1)}, u32[]{:S(2)}, u32[]{:S(2)}) async-start(s32[128,1,2]{2,1,0:T(1,128)} %bitcast.10), calls=%async_computation | async-start | bytes 131072 | tf_op jit(solution)/shard_map/all_to_all | solution.py:146
  92.3 7.0 %copy-start.5 = (f32[3,2048]{1,0:T(4,128)S(1)}, f32[3,2048]{1,0:T(4,128)}, u32[]{:S(2)}) copy-start(f32[3,2048]{1,0:T(4,128)} %param.18) | copy-start | bytes 73732
  92.3 7.1 %copy-start.6 = (f32[3,2048]{1,0:T(4,128)S(1)}, f32[3,2048]{1,0:T(4,128)}, u32[]{:S(2)}) copy-start(f32[3,2048]{1,0:T(4,128)} %param.19) | copy-start | bytes 73732
  92.3 7.2 %copy-start.2 = (bf16[256,456]{0,1:T(8,128)(2,1)S(1)}, bf16[256,456]{0,1:T(8,128)(2,1)}, u32[]{:S(2)}) copy-start(bf16[256,456]{0,1:T(8,128)(2,1)} %convolution_convert_fusion) | copy-start | bytes 700420
  92.3 8.2 %copy-start.10 = (s32[32,4]{0,1:T(4,128)S(1)}, s32[32,4]{0,1:T(4,128)}, u32[]{:S(2)}) copy-start(s32[32,4]{0,1:T(4,128)} %param.27) | copy-start | bytes 1540
  94.8 8.2 %all-to-all-start.3 = ((f32[4,4,456]{2,1,0:T(4,128)}), f32[4,4,456]{2,1,0:T(4,128)}, u32[]{:S(2)}, u32[]{:S(2)}) async-start(f32[4,4,456]{2,1,0:T(4,128)} %broadcast_in_dim.23), calls=%async_computation.3 | async-start | bytes 65536 | tf_op jit(solution)/shard_map/all_to_all | solution.py:18
  103.1 35.2 %all-to-all-start.1 = ((bf16[128,2,456]{2,1,0:T(2,128)(2,1)}), bf16[128,2,456]{2,1,0:T(2,128)(2,1)S(1)}, u32[]{:S(2)}, u32[]{:S(2)}) async-start(bf16[128,2,456]{2,1,0:T(2,128)(2,1)} %reshape.157), calls=%async_computation.1 | async-start | bytes 524288 | tf_op jit(solution)/shard_map/all_to_all | solution.py:139
  137.1 3.4 %copy-start.3 = (f32[3,152]{1,0:T(4,128)S(1)}, f32[3,152]{1,0:T(4,128)}, u32[]{:S(2)}) copy-start(f32[3,152]{1,0:T(4,128)} %constant.205) | copy-start | bytes 5476
where the time goes:
time: 156 us; the launch traced here: 155 us
  blocking collectives  53.1 us (34%)
  starting transfers between devices  43.1 us (28%)
  other arithmetic  26.7 us (17%)
  local copies, waits for them, and re-layouts  20.4 us (13%)
  matrix products  7.13 us (5%)
  waiting for transfers between devices  2.94 us (2%)
    all_gather x3, blocking collectives, all_blocks(): tiles = lax.all_gather(tiles, axes[k])  45.9 us
    all_to_all x1, starting transfers between devices, local(): lax.all_to_all(send_ids.reshape(leaf_count, capacity), LEAF, split_axis=0...  21 us
    all_to_all x1, starting transfers between devices, local(): lax.all_to_all(send_rows.reshape(leaf_count, capacity, width), LEAF, spli...  13.3 us
    reduce_sum x12, other arithmetic, stokes_apply(): squared = jnp.sum(relative * relative, axis=0)  9.54 us
    all_to_all x2, starting transfers between devices, sent_to_all(): lax.all_to_all(jnp.broadcast_to(value[None], (peers, *value.shape)), axis...  8.87 us
    all_to_all x1, blocking collectives, sent_to_all(): lax.all_to_all(jnp.broadcast_to(value[None], (peers, *value.shape)), axis...  7.21 us
    reduce_sum x8, other arithmetic, stokes_apply(): jnp.sum(weights * ((squared + 2.0 * EPSILON2) * spread + relative * along...  5.38 us
    gather x12, local copies, waits for them, and re-layouts, near_block(): return near_terms(here, points[:, chosen], vectors[:, chosen], moved)  4.93 us
  transfers between devices with their start and end apart: 4, of which 2 were waited for; matrix products, arithmetic and copies ran while one was open for 21% of the time, Pallas kernels for 0%

commit v1 on v0

v1 whole, which is shorter than its diff:
```python
import jax
import jax.numpy as jnp
import numpy as np
from jax import lax
from jax.experimental import pallas as pl
from jax.experimental.pallas import tpu as pltpu
from jax.sharding import PartitionSpec as P

SIDE = 6
EPS = 0.01
RADIUS = 0.525
M = 456
K = 152
NZ, NX, NL = 16, 8, 4
CH = 120
F32, BF16 = jnp.float32, jnp.bfloat16
MESH = pl.DeviceIdType.MESH


def surface_points():
    levels = np.linspace(-1.0, 1.0, SIDE)
    lattice = np.stack(np.meshgrid(levels, levels, levels, indexing="ij"), 0).reshape(3, -1)
    on_shell = np.max(np.abs(lattice), 0) > 1.0 - 1e-09
    return (lattice[:, on_shell] * RADIUS).astype(np.float32)


def iota(shape, dim):
    return lax.broadcasted_iota(jnp.int32, shape, dim)


def dot(a, b, dims=((1,), (0,))):
    return lax.dot_general(a, b, (dims, ((), ())), preferred_element_type=F32)


def one_hot(hits):
    return jnp.where(hits, 1.0, 0.0).astype(BF16)


def kernel(
    off, vel, m2l_h, child_h, cm_h, ids_ref, meta, shell, near_box, near_dir,
    out_ref,
    m2l, child, cm, cmt, x6, nat, tn, tab, xg, wst, qst, av, ppb, prs, idr, gz, pall, spb, spr,
    cpb, cpr, tms, sb, rb, fin, wt, fl, nn, fo, frb, frr,
    loc, ss, rs,
):
    me, lv = lax.axis_index("leaf"), lax.axis_index("lvl")
    zi, xi = me // NX, lax.rem(me, NX)

    def z_peer(k):
        return lax.rem(zi + k, NZ)

    def x_peer(k):
        return lax.rem(xi + k, NX)

    def y_peer(k):
        return lax.rem(lv + k, NL)

    barrier = pltpu.get_barrier_semaphore()

    def greet_z(k, c):
        pl.semaphore_signal(barrier, 1, device_id=(z_peer(k) * NX + xi, lv), device_id_type=MESH)
        return c

    def greet_x(k, c):
        pl.semaphore_signal(barrier, 1, device_id=(zi * NX + x_peer(k), lv), device_id_type=MESH)
        return c

    def greet_y(k, c):
        pl.semaphore_signal(barrier, 1, device_id=(me, y_peer(k)), device_id_type=MESH)
        return c

    lax.fori_loop(1, NZ, greet_z, 0)
    lax.fori_loop(1, NX, greet_x, 0)
    lax.fori_loop(1, NL, greet_y, 0)

    load_child = pltpu.make_async_copy(child_h, child, loc.at[0])
    load_m2l = pltpu.make_async_copy(m2l_h, m2l, loc.at[1])
    load_cm = pltpu.make_async_copy(cm_h, cm, loc.at[2])
    load_child.start()
    load_m2l.start()
    load_cm.start()

    def send(src, dst, phase, device):
        pltpu.make_async_remote_copy(
            src_ref=src, dst_ref=dst, send_sem=ss.at[phase], recv_sem=rs.at[phase],
            device_id=device, device_id_type=MESH,
        ).start()

    def arrived(ref, phase):
        pltpu.make_async_copy(ref, ref, rs.at[phase]).wait()

    def gone(ref, phase):
        pltpu.make_async_copy(ref, ref, ss.at[phase]).wait()

    x6[0:3] = off[...]
    x6[3:6] = vel[...]
    x6[6:8] = jnp.zeros((2, 2048), F32)
    low = iota((8, 128), 1) < 64
    for m in range(16):
        v = x6[:, m * 128 : (m + 1) * 128]
        nat[pl.ds(m, 8, stride=16), :] = v
        r = pltpu.roll(v, 64, 1)
        tab[2 * m] = jnp.where(low, v, r)
        tab[2 * m + 1] = jnp.where(low, r, v)
    tn[...] = nat[...].T
    lane16 = iota((16, 128), 1) // 16
    for c in range(6):
        total = jnp.zeros((16, 128), F32)
        for b2 in range(2):
            for g in range(4):
                j, pos = b2 * 4 + g, g * 2 + b2
                piece = pltpu.roll(tn[16 * j : 16 * j + 16, :], (16 * (pos - c)) % 128, 1)
                total = jnp.where(lane16 == pos, piece, total)
        xg[c] = total

    def to_surface(kb, carry):
        row = pl.multiple_of(kb * 8, 8)
        s = [shell[pl.ds(c * K + row, 8), :] for c in range(3)]
        acc = [jnp.zeros((8, 128), F32) for _ in range(3)]
        for i in range(16):
            r = [s[c] - xg[c, i : i + 1, :] for c in range(3)]
            v = [xg[3 + c, i : i + 1, :] for c in range(3)]
            t = r[0] * r[0] + r[1] * r[1] + r[2] * r[2] + EPS
            inv = lax.rsqrt(t)
            w = inv * inv * inv
            q = w * (t + EPS)
            wd = w * (r[0] * v[0] + r[1] * v[1] + r[2] * v[2])
            for c in range(3):
                acc[c] = acc[c] + (q * v[c] + wd * r[c])
            wst[i, pl.ds(row, 8), :] = w
            qst[i, pl.ds(row, 8), :] = q
        for c in range(3):
            av[pl.ds(c * K + row, 8), :] = acc[c]
        return carry

    lax.fori_loop(0, K // 8, to_surface, 0)
    a = av[...]
    a = a + pltpu.roll(a, 64, 1)
    a = a + pltpu.roll(a, 32, 1)
    b_row, b_lane = iota((32, 128), 0), iota((32, 128), 1)
    pick = one_hot(b_lane == lax.rem(b_row, 2) * 16 + b_row // 2)
    local = dot(pick, a.astype(BF16), ((1,), (1,))).astype(BF16)

    p_row, c_col = iota((8, 32), 0), iota((8, 32), 1)
    load_child.wait()
    part = jnp.zeros((8, M), F32)
    for o in range(2):
        rows = one_hot((c_col == p_row * 8 + lv * 2 + o) & (p_row < 4))
        part = part + dot(dot(rows, local).astype(BF16), child[o])
    ppb[3] = jnp.zeros((8, 128), F32)
    for k in range(3):
        ppb[k] = part[:, k * 128 : (k + 1) * 128]
    ppb[3, :, 0 : M - 384] = part[:, 384:M]
    pl.semaphore_wait(barrier, NZ + NX + NL - 3)
    for i in range(1, NL):
        send(ppb.at[y_peer(i)], prs.at[i - 1], 0, (me, y_peer(i)))
    for i in range(1, NL):
        send(ids_ref, idr.at[lv], 1, (me, y_peer(i)))
    idr[lv] = ids_ref[...]

    load_m2l.wait()
    tms[:, 384:512] = jnp.zeros((128, 128), F32)
    for c in range(4):
        tms[c * 32 : (c + 1) * 32, 0:M] = dot(local, m2l[c])
    own = jnp.broadcast_to(meta[0:1, :].astype(F32), (128, 128))
    place = jnp.broadcast_to(meta[1:2, :].astype(F32), (128, 128)).T
    sub, lane = iota((128, 128), 0), iota((128, 128), 1)
    rank = jnp.sum(jnp.where((own.T == own) & (sub < lane), 1.0, 0.0), axis=0, keepdims=True)
    pos = (meta[0:1, :] * 2 + rank.astype(jnp.int32)) * 4
    keys = jnp.concatenate([pos + j for j in range(4)], axis=1)
    flat = tms[...]
    pieces = []
    for j in range(4):
        piece = flat if j == 0 else pltpu.roll(flat, 512 - CH * j, 1)
        piece = jnp.where(lane < CH, piece[:, 0:128], jnp.where(lane == 127, place + 1.0, 0.0))
        pieces.append(piece.astype(BF16))
    pieces = jnp.concatenate(pieces, axis=0)
    for q in range(4):
        hits = one_hot(iota((256, 512), 0) + q * 256 == keys)
        sb[q * 4 : (q + 1) * 4] = dot(hits, pieces).reshape(4, 8, 8, 128).astype(BF16)
    rb[15] = sb[zi]

    arrived(prs, 0)
    mine = ppb[lv] + prs[0] + prs[1] + prs[2]
    gz[zi] = mine.astype(BF16)

    def gather_z(k, c):
        send(gz.at[zi], gz.at[zi], 2, (z_peer(8 - k) * NX + xi, lv))
        return c

    def gather_z2(k, c):
        send(gz.at[zi], gz.at[zi], 2, (z_peer(8 + k) * NX + xi, lv))
        return c

    lax.fori_loop(0, 8, gather_z, 0)
    lax.fori_loop(1, 8, gather_z2, 0)

    def leaf_z(k, c):
        send(sb.at[z_peer(8 - k)], rb.at[2 * k], 3, (z_peer(8 - k) * NX + xi, lv))
        send(sb.at[z_peer(8 + k)], rb.at[2 * k - 1], 3, (z_peer(8 + k) * NX + xi, lv))
        return c

    send(sb.at[z_peer(8)], rb.at[0], 3, (z_peer(8) * NX + xi, lv))
    lax.fori_loop(1, 8, leaf_z, 0)

    row8 = iota((8, 128), 0)
    lane_t = iota((64, 128), 1)

    def near(m, carry):
        turned = pltpu.roll(tn[...], 128 - m, 1)
        columns = []
        for b2 in range(2):
            box = 2 * m + b2
            sources = []
            for pair in range(2):
                n1, n2 = 2 * pair, 2 * pair + 1
                d1, d2 = near_dir[box, n1], near_dir[box, n2]
                moved = jnp.where(low, tab[near_box[box, n1]], tab[near_box[box, n2]])
                parts = [(d // 9 - 1, lax.rem(d // 3, 3) - 1, lax.rem(d, 3) - 1) for d in (d1, d2)]
                shift = jnp.zeros((8, 128), F32)
                for c in range(3):
                    both = jnp.where(low, parts[0][c].astype(F32), parts[1][c].astype(F32))
                    shift = jnp.where(row8 == c, both, shift)
                moved = moved + shift
                sources.append([jnp.broadcast_to(moved[c : c + 1, :], (8, 128)) for c in range(6)])
            sums = [[], [], []]
            for tv in range(8):
                at = b2 * 64 + tv * 8
                x = [
                    jnp.broadcast_to(turned[at : at + 8, 16 * c : 16 * c + 1], (8, 128))
                    for c in range(3)
                ]
                acc = [jnp.zeros((8, 128), F32) for _ in range(3)]
                for pair in range(2):
                    src = sources[pair]
                    r = [x[c] - src[c] for c in range(3)]
                    t = r[0] * r[0] + r[1] * r[1] + r[2] * r[2] + EPS
                    inv = lax.rsqrt(t)
                    w = inv * inv * inv
                    q = w * (t + EPS)
                    wd = w * (r[0] * src[3] + r[1] * src[4] + r[2] * src[5])
                    for c in range(3):
                        acc[c] = acc[c] + (q * src[3 + c] + wd * r[c])
                column = [jnp.sum(acc[c], axis=1, keepdims=True) for c in range(3)]
                columns.append(
                    jnp.where(
                        iota((8, 128), 1) == 0,
                        column[0],
                        jnp.where(iota((8, 128), 1) == 1, column[1], column[2]),
                    )
                )
        turned_back = jnp.concatenate(columns, axis=0).T
        for c in range(3):
            nn[c, pl.ds(m, 1), :] = turned_back[c : c + 1, :]
        return carry

    lax.fori_loop(0, 16, near, 0)

    load_cm.wait()
    wt[...] = jnp.zeros((512, 512), F32)
    wt[0:M, 0:M] = cm[...]
    cmt[...] = wt[...].T.astype(BF16)

    arrived(gz.at[pl.ds(0, NZ - 1)], 2)
    for i in range(1, NX):
        send(gz, pall.at[xi], 4, (zi * NX + x_peer(i), lv))
    pall[xi] = gz[...]
    arrived(idr.at[pl.ds(0, NL - 1)], 1)
    parents = iota((8, 1024), 0)
    wanted = jnp.where(parents < 4, me * 4 + parents, -2)
    selects = []
    for l in range(NL):
        for c in range(4):
            selects.append(jnp.where(idr[l, c : c + 1, :] == wanted, 1.0, 0.0))
    select = jnp.concatenate(selects, axis=0).astype(BF16)
    arrived(pall.at[pl.ds(0, NX - 1)], 4)
    coarse = pall[...].astype(F32).reshape(1024, 128).astype(BF16)
    spb[...] = dot(select, coarse).reshape(4, 32, 128).astype(BF16)
    for i in range(1, NL):
        send(spb.at[y_peer(i)], spr.at[lv], 5, (me, y_peer(i)))
    spr[lv] = spb[lv]

    arrived(rb.at[pl.ds(0, NZ - 1)], 3)
    for i in range(1, NX):
        send(rb.at[:, x_peer(i)], fin.at[i - 1], 6, (zi * NX + x_peer(i), lv))
    fin[7] = rb[:, xi]

    arrived(spr.at[pl.ds(0, NL - 1)], 5)
    rows = jnp.concatenate([spr[k].astype(F32) for k in range(4)], axis=1)
    part = jnp.zeros((8, M), F32)
    for c in range(4):
        part = part + dot(rows[c * 8 : (c + 1) * 8, 0:M].astype(BF16), m2l[c])
    cpb[...] = 0.5 * part
    for i in range(1, NL):
        send(cpb, cpr.at[i - 1], 7, (me, y_peer(i)))
    arrived(cpr, 7)
    parent = cpb[...] + cpr[0] + cpr[1] + cpr[2]

    def box_of(lanes):
        beta = lax.rem(lanes, 32)
        return 2 * lax.rem(beta, 16) + beta // 16

    p_box = box_of(iota((8, 128), 1))
    lowered = jnp.zeros((M, 128), F32)
    for o in range(2):
        spread = one_hot((p_box // 8 == row8) & (lax.rem(p_box, 8) == lv * 2 + o))
        lowered = lowered + dot(child[o], dot(parent.astype(BF16), spread, ((0,), (0,))).astype(BF16))

    arrived(fin.at[pl.ds(0, NX - 1)], 6)
    got = fin[...].astype(F32).reshape(1024, 128)
    ident = got[:, 127:128]
    quarter = lax.rem(iota((1024, 1), 0), 4).astype(F32)
    key = jnp.where(ident > 0.5, ident - 1.0 + 32.0 * quarter, -1.0)
    landing = one_hot(key.astype(jnp.int32) == iota((1024, 128), 1))
    landed = dot(got.astype(BF16), landing, ((0,), (0,))).astype(BF16)
    e_box = box_of(lane)
    totals = [dot(landed[0:CH, :], one_hot(sub == 32 * j + e_box)) for j in range(4)]
    total = jnp.concatenate(totals, axis=0)[0:M, :] + lowered
    fl[...] = dot(cmt[0:M, 0:M], total.astype(BF16))

    def from_surface(i, carry):
        x = [jnp.broadcast_to(xg[c, pl.ds(i, 1), :], (8, 128)) for c in range(3)]
        acc = [jnp.zeros((8, 128), F32) for _ in range(3)]
        for kb in range(K // 8):
            at = kb * 8
            f = [fl[c * K + at : c * K + at + 8, :] for c in range(3)]
            r = [x[c] - shell[c * K + at : c * K + at + 8, :] for c in range(3)]
            q = qst[i, at : at + 8, :]
            wd = wst[i, at : at + 8, :] * (r[0] * f[0] + r[1] * f[1] + r[2] * f[2])
            for c in range(3):
                acc[c] = acc[c] + (q * f[c] + wd * r[c])
        for c in range(3):
            fo[pl.ds(c * 16 + i, 1), :] = jnp.sum(acc[c], axis=0, keepdims=True)
        return carry

    fo[48:128] = jnp.zeros((80, 128), F32)
    lax.fori_loop(0, 16, from_surface, 0)
    back = fo[...].T
    for c in range(3):
        total = jnp.zeros((16, 128), F32)
        for b2 in range(2):
            for g in range(4):
                at = g * 32 + b2 * 16
                pos = b2 * 4 + g
                piece = pltpu.roll(back[at : at + 16, :], (16 * (pos - c)) % 128, 1)
                total = jnp.where(lane16 == pos, piece, total)
        frb[c] = total + nn[c]
    for i in range(1, NL):
        send(frb, frr.at[i - 1], 8, (me, y_peer(i)))
    arrived(frr, 8)
    out_ref[...] = frb[...] + frr[0] + frr[1] + frr[2]

    gone(ppb.at[pl.ds(0, NL - 1)], 0)
    gone(idr.at[pl.ds(0, NL - 1)], 1)
    gone(gz.at[pl.ds(0, NZ - 1)], 2)
    gone(rb.at[pl.ds(0, NZ - 1)], 3)
    gone(pall.at[pl.ds(0, NX - 1)], 4)
    gone(spb.at[pl.ds(0, NL - 1)], 5)
    gone(fin.at[pl.ds(0, NX - 1)], 6)
    gone(cpr, 7)
    gone(frr, 8)


def local_part(
    offsets, vel_cot, m2l_ops, child_ops, check_map, leaf_dest, leaf_slot, coarse_dest,
    coarse_slot, near_box, near_dir,
):
    shell = jnp.asarray(np.repeat(surface_points().reshape(M, 1), 128, axis=1))
    ids = (coarse_dest[0, :, :, 0] * 4 + coarse_slot[0]).reshape(NZ, NX, 4, 4)
    ids = ids.transpose(3, 1, 0, 2)
    ids = jnp.pad(ids, ((0, 4), (0, 0), (0, 0), (0, 4)), constant_values=-1).reshape(8, 1024)
    meta = jnp.stack([leaf_dest[0, :, :, 0].T.reshape(128), leaf_slot[0].T.reshape(128)])
    vmem = pl.BlockSpec(memory_space=pltpu.VMEM)
    hbm = pl.BlockSpec(memory_space=pl.ANY)
    smem = pl.BlockSpec(memory_space=pltpu.SMEM)
    V = pltpu.VMEM
    out = pl.pallas_call(
        kernel,
        out_shape=jax.ShapeDtypeStruct((3, 16, 128), F32),
        in_specs=[vmem, vmem, hbm, hbm, hbm, vmem, vmem, vmem, smem, smem],
        out_specs=vmem,
        scratch_shapes=[
            V((4, M, M), BF16), V((2, M, M), BF16), V((M, M), F32), V((512, 512), BF16),
            V((8, 2048), F32), V((128, 128), F32), V((128, 128), F32), V((32, 8, 128), F32),
            V((6, 16, 128), F32), V((16, K, 128), F32), V((16, K, 128), F32), V((M, 128), F32),
            V((4, 8, 128), F32), V((3, 8, 128), F32), V((4, 8, 1024), jnp.int32),
            V((NZ, 8, 128), BF16), V((NX, NZ, 8, 128), BF16), V((4, 32, 128), BF16),
            V((4, 32, 128), BF16), V((8, M), F32), V((3, 8, M), F32), V((128, 512), F32),
            V((NZ, NX, 8, 128), BF16), V((NZ, NX, 8, 128), BF16), V((NX, NZ, 8, 128), BF16),
            V((512, 512), F32), V((M, 128), F32), V((3, 16, 128), F32), V((128, 128), F32),
            V((3, 16, 128), F32), V((3, 3, 16, 128), F32),
            pltpu.SemaphoreType.DMA((3,)), pltpu.SemaphoreType.DMA((9,)),
            pltpu.SemaphoreType.DMA((9,)),
        ],
        compiler_params=pltpu.CompilerParams(collective_id=0, has_side_effects=True),
    )(offsets, vel_cot, m2l_ops, child_ops, check_map, ids, meta, shell, near_box, near_dir)
    return out.reshape(3, 2048)


def solution(mesh):
    return jax.shard_map(
        local_part,
        mesh=mesh,
        in_specs=(
            P(None, "leaf"), P(None, "leaf"), P("lvl", None, None), P("lvl", None, None), P(),
            P("lvl", "leaf", None, None), P("lvl", "leaf", None), P("lvl", None, None, None),
            P("lvl", None, None), P("leaf", "lvl"), P("leaf", "lvl"),
        ),
        out_specs=P(None, "leaf"),
        check_vma=False,
    )
```

time: 156 us -> 67.1 us (0.43)
  Pallas kernels: 0 us -> 59.8 us
  blocking collectives: 53.1 us -> 0 us
  starting transfers between devices: 43.1 us -> 0 us
  other arithmetic: 26.7 us -> 1.39 us
  local copies, waits for them, and re-layouts: 20.4 us -> 5.1 us
  matrix products: 7.13 us -> 0 us
  waiting for transfers between devices: 2.94 us -> 0 us
    pallas_call x0 -> x1, Pallas kernels: none -> 59.8 us  [local_part(): pl.pallas_call(kernel, out_shape=jax.ShapeDtypeStruct((3, 16, 128), F32),...]
    all_gather x3 -> x0, blocking collectives: 45.9 us -> none  [all_blocks(): tiles = lax.all_gather(tiles, axes[k])]
    all_to_all x4 -> x0, starting transfers between devices: 43.1 us -> none  [the longest x1 21 us: local(): lax.all_to_all(send_ids.reshape(leaf_count, capacity), LEAF, split_axis=0...]
    reduce_sum x28 -> x0, other arithmetic: 21.2 us -> none  [the longest x12 9.54 us: stokes_apply(): squared = jnp.sum(relative * relative, axis=0)]
    all_to_all x1 -> x0, blocking collectives: 7.21 us -> none  [sent_to_all(): lax.all_to_all(jnp.broadcast_to(value[None], (peers, *value.shape)), axis...]
    dot_general x9 -> x0, matrix products: 7.13 us -> none  [the longest x1 1.85 us: local(): jnp.einsum('cpr,crn->pn', select, terms, precision=lax.Precision.HIGHEST)]
    gather x12 -> x0, local copies, waits for them, and re-layouts: 4.93 us -> none  [near_block(): return near_terms(here, points[:, chosen], vectors[:, chosen], moved)]
    another operation x10 -> x2, local copies, waits for them, and re-layouts: 3.51 us -> 0.16 us  [local_part(): jnp.stack([leaf_dest[0, :, :, 0].T.reshape(128), leaf_slot[0].T.reshape(1...]
  transfers between devices with their start and end apart: 4 -> 0, of which waited for: 2 -> 0; matrix products, arithmetic and copies ran while one was open for 21% -> 0% of each run, Pallas kernels for 0% -> 0%
where the time goes in v1:
time: 67.1 us; the launch traced here: 66.4 us
  Pallas kernels  59.8 us (89%)
  local copies, waits for them, and re-layouts  5.1 us (8%)
  other arithmetic  1.39 us (2%)
    pallas_call x1, Pallas kernels, local_part(): pl.pallas_call(kernel, out_shape=jax.ShapeDtypeStruct((3, 16, 128), F32),...  59.8 us
    unnamed x12, local copies, waits for them, and re-layouts  2.8 us

profile of v1, /device:TPU:1, one launch (start us, length us, event | category | flops | bytes accessed | tf_op | source)
XLA Modules:
  0.0 66.4 jit_solution(38594014368531732)
XLA Ops:
  0.0 0.0 copy-start
  0.0 0.0 copy-start.1
  0.0 0.0 copy-start.2
  0.0 0.0 copy-start.3
  0.0 0.8 %multiply_reduce_fusion = s32[512,4]{0,1:T(4,128)S(1)} fusion(s32[1,512,4,1]{1,3,2,0:T(1,128)} %param.19), kind=kLoop, calls=%fused_computation.2 | loop fusion | flops 2048 | bytes 16384 | tf_op jit(solution)/shard_map/mul | solution.py:369
  0.8 0.3 mul.12
  1.1 1.0 %squeeze.10 = s32[16,8,4,4]{2,1,0,3:T(8,128)S(1)} reshape(s32[1,512,4]{1,2,0:T(4,128)} %param.20) | data formatting | bytes 16384 | tf_op jit(solution)/shard_map/squeeze | solution.py:369
  2.2 0.9 %reshape.11.ids_ref = s32[8,1024]{1,0:T(8,128)} reshape(s32[8,8,16,8]{3,2,1,0:T(8,128)S(1)} %pad.4.clone) | data formatting | bytes 65536 | tf_op jit(solution)/shard_map/reshape | solution.py:371
  3.0 0.0 copy-done
  3.1 0.7 %copy.18.near_box = s32[32,4]{1,0:T(8,128)} copy(s32[32,4]{0,1:T(4,128)S(1)} %copy-done) | data formatting | bytes 1024 | tf_op args[9]
  3.7 0.0 copy-done.1
  3.7 0.7 %copy.19.near_dir = s32[32,4]{1,0:T(8,128)} copy(s32[32,4]{0,1:T(4,128)S(1)} %copy-done.1) | data formatting | bytes 1024 | tf_op args[10]
  4.4 0.0 copy-done.2
  4.4 0.1 stack_reshape.6
  4.5 0.0 copy-done.3
  4.5 0.1 stack_reshape.7
  4.6 0.6 pad_add_fusion.meta
  5.2 59.8 %shard_map.118 = f32[3,16,128]{2,1,0:T(8,128)} custom-call(f32[3,2048]{1,0:T(4,128)} %off.1, f32[3,2048]{1,0:T(4,128)} %vel.1, bf16[4,456,456]{2,1,0:T(8,128)(2,1)} %m2l_h.1, bf16[2,456,456]{2,1,0:T(8,128)(2,1)} %child_h.1, f32[456,456]{1,0:T(8,128)} %cm_h.1, s32[8,1024]{1,0:T(8,128)} %reshape.11.ids_ref, s32[2,128]{1,0:T(2,128)} %pad_add_fusion.meta, ...), custom_call_target="tpu_custom_call" | custom-call | tf_op jit(solution)/shard_map/pallas_call | solution.py:377
  65.0 1.4 %copy.23 = f32[1,3,16,128]{3,1,2,0:T(4,128)} copy(f32[1,3,16,128]{3,2,1,0:T(8,128)} %bitcast.18) | data formatting | bytes 49152
  (3 shorter events, 0.1 us)
Async XLA Ops:
  0.0 3.1 %copy-start = (s32[32,4]{0,1:T(4,128)S(1)}, s32[32,4]{0,1:T(4,128)}, u32[]{:S(2)}) copy-start(s32[32,4]{0,1:T(4,128)} %param.21) | copy-start | bytes 1540
  0.0 3.7 %copy-start.1 = (s32[32,4]{0,1:T(4,128)S(1)}, s32[32,4]{0,1:T(4,128)}, u32[]{:S(2)}) copy-start(s32[32,4]{0,1:T(4,128)} %param.22) | copy-start | bytes 1540
  0.0 4.4 %copy-start.2 = (s32[1,32,4,1]{1,3,2,0:T(1,128)S(1)}, s32[1,32,4,1]{1,3,2,0:T(1,128)}, u32[]{:S(2)}) copy-start(s32[1,32,4,1]{1,3,2,0:T(1,128)} %param.17) | copy-start | bytes 1540
  0.0 4.5 %copy-start.3 = (s32[1,32,4]{1,2,0:T(4,128)S(1)}, s32[1,32,4]{1,2,0:T(4,128)}, u32[]{:S(2)}) copy-start(s32[1,32,4]{1,2,0:T(4,128)} %param.18) | copy-start | bytes 1540

commit v2 on v1

v2 whole, which is shorter than its diff:
```python
import jax
import jax.numpy as jnp
import numpy as np
from jax import lax
from jax.experimental import pallas as pl
from jax.experimental.pallas import tpu as pltpu
from jax.sharding import PartitionSpec as P

SIDE = 6
EPS = 0.01
RADIUS = 0.525
M = 456
K = 152
NZ, NX, NL = 16, 8, 4
CH = 120
NEAREST = 2
F32, BF16, I32 = jnp.float32, jnp.bfloat16, jnp.int32
MESH = pl.DeviceIdType.MESH


def surface_points():
    levels = np.linspace(-1.0, 1.0, SIDE)
    lattice = np.stack(np.meshgrid(levels, levels, levels, indexing="ij"), 0).reshape(3, -1)
    on_shell = np.max(np.abs(lattice), 0) > 1.0 - 1e-09
    return (lattice[:, on_shell] * RADIUS).astype(np.float32)


def iota(shape, dim):
    return lax.broadcasted_iota(jnp.int32, shape, dim)


def dot(a, b, dims=((1,), (0,))):
    return lax.dot_general(a, b, (dims, ((), ())), preferred_element_type=F32)


def one_hot(hits):
    return jnp.where(hits, 1.0, 0.0).astype(BF16)


def kernel(
    off_h, vel_h, shell_h, leaf_dest_h, leaf_slot_h, coarse_dest_h, coarse_slot_h, near_box_h,
    near_dir_h, child_h, m2l_h, cm_h, out_ref,
    off, vel, shell, leaf_dest, leaf_slot, coarse_dest, coarse_slot, near_box, near_dir,
    m2l, child, cm, cmt, down, x6, nat, tn, thirds, tab, xg, wst, qst, av, ppb, prs, ids, gz, pall, spb, spr,
    cpb, cpr, meta, tms, sb, rb, fin, wt, fl, nn, fo, frb, frs, frr,
    loc, ss, rs,
):
    me, lv = lax.axis_index("leaf"), lax.axis_index("lvl")
    zi, xi = me // NX, lax.rem(me, NX)

    def z_peer(k):
        return lax.rem(zi + k, NZ)

    def x_peer(k):
        return lax.rem(xi + k, NX)

    def y_peer(k):
        return lax.rem(lv + k, NL)

    barrier = pltpu.get_barrier_semaphore()

    def greet_z(k, c):
        pl.semaphore_signal(barrier, 1, device_id=(z_peer(k) * NX + xi, lv), device_id_type=MESH)
        return c

    def greet_x(k, c):
        pl.semaphore_signal(barrier, 1, device_id=(zi * NX + x_peer(k), lv), device_id_type=MESH)
        return c

    def greet_y(k, c):
        pl.semaphore_signal(barrier, 1, device_id=(me, y_peer(k)), device_id_type=MESH)
        return c

    lax.fori_loop(1, NZ, greet_z, 0)
    lax.fori_loop(1, NX, greet_x, 0)
    lax.fori_loop(1, NL, greet_y, 0)

    loads = [
        pltpu.make_async_copy(src, dst, loc.at[n])
        for n, (src, dst) in enumerate(
            (
                (off_h, off), (vel_h, vel), (shell_h, shell), (leaf_dest_h, leaf_dest),
                (leaf_slot_h, leaf_slot), (coarse_dest_h, coarse_dest),
                (coarse_slot_h, coarse_slot), (near_box_h, near_box), (near_dir_h, near_dir),
                (child_h, child), (m2l_h, m2l), (cm_h, cm),
            )
        )
    ]
    for load in loads:
        load.start()

    def send(src, dst, phase, device):
        pltpu.make_async_remote_copy(
            src_ref=src, dst_ref=dst, send_sem=ss.at[phase], recv_sem=rs.at[phase],
            device_id=device, device_id_type=MESH,
        ).start()

    def arrived(ref, phase):
        pltpu.make_async_copy(ref, ref, rs.at[phase]).wait()

    def gone(ref, phase):
        pltpu.make_async_copy(ref, ref, ss.at[phase]).wait()

    groups = ((0, 6), (6, 6), (12, 4))

    def group_of(slot):
        return 3 if slot < 6 else 9 if slot < 12 else 10

    def forward(g):
        first, count = groups[g]
        arrived(rb.at[pl.ds(first, count - (g == 2))], group_of(first))
        for i in range(1, NX):
            src, dst = rb.at[pl.ds(first, count), x_peer(i)], fin.at[i - 1, pl.ds(first, count)]
            send(src, dst, 11 if g == 2 else 6, (zi * NX + x_peer(i), lv))

    for load in loads[0:3]:
        load.wait()
    x6[0:3] = off[...]
    x6[3:6] = vel[...]
    x6[6:8] = jnp.zeros((2, 2048), F32)
    low = iota((8, 128), 1) < 64
    for m in range(16):
        v = x6[:, m * 128 : (m + 1) * 128]
        nat[pl.ds(m, 8, stride=16), :] = v
        r = pltpu.roll(v, 64, 1)
        tab[2 * m] = jnp.where(low, v, r)
        tab[2 * m + 1] = jnp.where(low, r, v)
    tn[...] = nat[...].T
    lane16 = iota((16, 128), 1) // 16
    for c in range(3):
        whole = tn[...] if c == 0 else pltpu.roll(tn[...], 128 - 16 * c, 1)
        whole = jnp.where(iota((128, 128), 1) < 16, whole, 0.0)
        high = whole.astype(BF16).astype(F32)
        middle = (whole - high).astype(BF16).astype(F32)
        lowest = whole - high - middle
        split = high + pltpu.roll(middle, 16, 1) + pltpu.roll(lowest, 32, 1)
        thirds[c * 128 : (c + 1) * 128, :] = split.astype(BF16)
    for c in range(6):
        total = jnp.zeros((16, 128), F32)
        for b2 in range(2):
            for g in range(4):
                j, pos = b2 * 4 + g, g * 2 + b2
                piece = pltpu.roll(tn[16 * j : 16 * j + 16, :], (16 * (pos - c)) % 128, 1)
                total = jnp.where(lane16 == pos, piece, total)
        xg[c] = total

    def to_surface(kb, carry):
        row = pl.multiple_of(kb * 8, 8)
        s = [shell[pl.ds(c * K + row, 8), :] for c in range(3)]
        acc = [jnp.zeros((8, 128), F32) for _ in range(3)]
        for i in range(16):
            r = [s[c] - xg[c, i : i + 1, :] for c in range(3)]
            v = [xg[3 + c, i : i + 1, :] for c in range(3)]
            t = r[0] * r[0] + r[1] * r[1] + r[2] * r[2] + EPS
            inv = lax.rsqrt(t)
            w = inv * inv * inv
            q = w * (t + EPS)
            wd = w * (r[0] * v[0] + r[1] * v[1] + r[2] * v[2])
            for c in range(3):
                acc[c] = acc[c] + (q * v[c] + wd * r[c])
            wst[i, pl.ds(row, 8), :] = w
            qst[i, pl.ds(row, 8), :] = q
        for c in range(3):
            av[pl.ds(c * K + row, 8), :] = acc[c]
        return carry

    lax.fori_loop(0, K // 8, to_surface, 0)
    a = av[...]
    a = a + pltpu.roll(a, 64, 1)
    a = a + pltpu.roll(a, 32, 1)
    b_row, b_lane = iota((32, 128), 0), iota((32, 128), 1)
    pick = one_hot(b_lane == lax.rem(b_row, 2) * 16 + b_row // 2)
    local = dot(pick, a.astype(BF16), ((1,), (1,))).astype(BF16)

    for load in loads[3:7]:
        load.wait()
    for c in range(4):
        ids[lv, c : c + 1, :] = coarse_dest[c].astype(F32)
    ids[lv, 4:8, :] = coarse_slot[...].astype(F32)
    meta[...] = jnp.zeros((8, 128), F32)
    for c in range(4):
        meta[c : c + 1, 0:32] = leaf_dest[c].astype(F32)
    meta[4:8, 0:32] = leaf_slot[...].astype(F32)

    p_row, c_col = iota((8, 32), 0), iota((8, 32), 1)
    loads[9].wait()
    part = jnp.zeros((8, M), F32)
    for o in range(2):
        rows = one_hot((c_col == p_row * 8 + lv * 2 + o) & (p_row < 4))
        part = part + dot(dot(rows, local).astype(BF16), child[o])
    ppb[3] = jnp.zeros((8, 128), F32)
    for k in range(3):
        ppb[k] = part[:, k * 128 : (k + 1) * 128]
    ppb[3, :, 0 : M - 384] = part[:, 384:M]
    pl.semaphore_wait(barrier, NZ + NX + NL - 3)
    for i in range(1, NL):
        send(ppb.at[y_peer(i)], prs.at[i - 1], 0, (me, y_peer(i)))
    for i in range(1, NL):
        send(ids.at[lv], ids.at[lv], 1, (me, y_peer(i)))

    loads[10].wait()
    tms[:, 384:512] = jnp.zeros((128, 128), F32)
    for c in range(4):
        tms[c * 32 : (c + 1) * 32, 0:M] = dot(local, m2l[c])
    lane32 = iota((1, 128), 1) // 32
    listed = []
    for first in (0, 4):
        line = meta[first : first + 1, :]
        for c in range(1, 4):
            line = jnp.where(lane32 == c, pltpu.roll(meta[first + c : first + c + 1, :], 32 * c, 1), line)
        listed.append(line)
    own = jnp.broadcast_to(listed[0], (128, 128))
    place = jnp.broadcast_to(listed[1], (128, 128)).T
    sub, lane = iota((128, 128), 0), iota((128, 128), 1)
    rank = jnp.sum(jnp.where((own.T == own) & (sub < lane), 1.0, 0.0), axis=0, keepdims=True)
    pos = (listed[0] * 2.0 + rank).astype(jnp.int32) * 4
    keys = jnp.concatenate([pos + j for j in range(4)], axis=1)
    flat = tms[...]
    pieces = []
    for j in range(4):
        piece = flat if j == 0 else pltpu.roll(flat, 512 - CH * j, 1)
        piece = jnp.where(lane < CH, piece[:, 0:128], jnp.where(lane == 127, place + 1.0, 0.0))
        pieces.append(piece.astype(BF16))
    pieces = jnp.concatenate(pieces, axis=0)
    for q in range(4):
        hits = one_hot(iota((256, 512), 0) + q * 256 == keys)
        sb[q * 4 : (q + 1) * 4] = dot(hits, pieces).reshape(4, 8, 8, 128).astype(BF16)
    rb[15] = sb[zi]

    def leaf_z(first, last):
        for slot in range(first, last):
            k = 1 + slot // 2 if slot % 2 == 0 else NZ - 1 - slot // 2
            send(sb.at[z_peer(k)], rb.at[slot], group_of(slot), (z_peer(k) * NX + xi, lv))

    leaf_z(0, NEAREST)

    arrived(prs, 0)
    mine = ppb[lv] + prs[0] + prs[1] + prs[2]
    gz[4] = mine[0:4].astype(BF16)
    for k in (8, 7, 9, 6, 10, 5, 11, 4, 12, 3, 13, 2, 14, 1, 15):
        slot = (4 - k) % NZ
        send(gz.at[4], gz.at[slot], 2 if slot < 9 else 12, (z_peer(k) * NX + xi, lv))
    leaf_z(NEAREST, 15)

    row8 = iota((8, 128), 0)
    loads[7].wait()
    loads[8].wait()

    def digits(code):
        by9, by3 = (code * 57) >> 9, (code * 43) >> 7
        return by9 - 1, by3 - 3 * by9 - 1, code - 3 * by3 - 1

    def near(m, carry):
        chosen = one_hot(lax.rem(iota((48, 128), 0), 16) == m)
        targets = dot(thirds[:, 0:48], chosen)
        columns = [[], [], []]
        for b2 in range(2):
            box = 2 * m + b2
            sources = []
            for pair in range(2):
                n1, n2 = 2 * pair, 2 * pair + 1
                d1, d2 = near_dir[n1, box], near_dir[n2, box]
                moved = jnp.where(low, tab[near_box[n1, box]], tab[near_box[n2, box]])
                parts = [digits(d) for d in (d1, d2)]
                shift = jnp.zeros((8, 128), F32)
                for c in range(3):
                    both = jnp.where(low, parts[0][c].astype(F32), parts[1][c].astype(F32))
                    shift = jnp.where(row8 == c, both, shift)
                moved = moved + shift
                sources.append([jnp.broadcast_to(moved[c : c + 1, :], (8, 128)) for c in range(6)])
            for tv in range(8):
                at = b2 * 64 + tv * 8
                x = [targets[c * 128 + at : c * 128 + at + 8, :] for c in range(3)]
                acc = [jnp.zeros((8, 128), F32) for _ in range(3)]
                for src in sources:
                    r = [x[c] - src[c] for c in range(3)]
                    t = r[0] * r[0] + r[1] * r[1] + r[2] * r[2] + EPS
                    inv = lax.rsqrt(t)
                    w = inv * inv * inv
                    q = w * (t + EPS)
                    wd = w * (r[0] * src[3] + r[1] * src[4] + r[2] * src[5])
                    for c in range(3):
                        acc[c] = acc[c] + (q * src[3 + c] + wd * r[c])
                for c in range(3):
                    columns[c].append(acc[c])
        for c in range(3):
            total = jnp.concatenate(columns[c], axis=0)
            high = total.astype(BF16)
            rest = (total - high.astype(F32)).astype(BF16)
            both = jnp.concatenate([high, rest], axis=1)
            nn[c, pl.ds(m, 1), :] = dot(jnp.ones((8, 256), BF16), both, ((1,), (1,)))[0:1, :]
        return carry

    lax.fori_loop(0, 16, near, 0, unroll=2)

    loads[11].wait()
    wt[...] = jnp.zeros((512, 512), F32)
    wt[0:M, 0:M] = cm[...]
    cmt[...] = wt[...].T.astype(BF16)

    for first, count, phase in ((0, 9, 2), (9, 7, 12)):
        arrived(gz.at[pl.ds(first, min(count, 8))], phase)
        for i in range(1, NX):
            part = gz.at[pl.ds(first, count)]
            send(part, pall.at[xi, pl.ds(first, count)], 4, (zi * NX + x_peer(i), lv))
    pall[xi] = gz[...]
    for o in range(2):
        down[o] = dot(cmt[0:M, 0:M], child[o]).astype(BF16)
    arrived(ids.at[pl.ds(0, NL - 1)], 1)
    col = iota((512, 512), 1)
    plane = lax.rem(zi + lax.rem(col // 4, NZ) + 12, NZ)
    gathered = (plane * NX + col // 64) * 4 + lax.rem(col, 4)
    order = one_hot(iota((512, 512), 0) == gathered)
    listed = dot(ids[...].reshape(32, 512).astype(BF16), order)
    parents = iota((8, 512), 0)
    wanted = (me * 4 + lax.rem(parents, 4)).astype(F32)
    selects = []
    for l in range(NL):
        for c in (0, 2):
            first, second = (
                listed[8 * l + n : 8 * l + n + 1, :] * 4.0 + listed[8 * l + 4 + n : 8 * l + 5 + n, :]
                for n in (c, c + 1)
            )
            named = jnp.where(parents < 4, first, second)
            selects.append(jnp.where(named == wanted, 1.0, 0.0))
    select = jnp.concatenate(selects, axis=0).astype(BF16)
    forward(0)
    arrived(pall.at[pl.ds(0, NX - 1)], 4)
    coarse = [
        jnp.concatenate([pall[x, 2 * z].astype(F32), pall[x, 2 * z + 1].astype(F32)], axis=0)
        for x in range(NX)
        for z in range(NZ // 2)
    ]
    coarse = jnp.concatenate(coarse, axis=0).astype(BF16)
    spb[...] = dot(select, coarse).reshape(4, 16, 128).astype(BF16)
    for i in range(1, NL):
        send(spb.at[y_peer(i)], spr.at[lv], 5, (me, y_peer(i)))
    spr[lv] = spb[lv]

    forward(1)

    arrived(spr.at[pl.ds(0, NL - 1)], 5)
    rows = jnp.concatenate([spr[k].astype(F32) for k in range(4)], axis=1)[:, 0:M]
    part = jnp.zeros((16, M), F32)
    for c in range(4):
        part = part + dot(jnp.where(iota((16, M), 0) // 4 == c, rows, 0.0).astype(BF16), m2l[c])
    part = part[0:8] + part[8:16]
    cpb[...] = 0.5 * (part[0:4] + part[4:8])
    for i in range(1, NL):
        send(cpb, cpr.at[i - 1], 7, (me, y_peer(i)))
    forward(2)
    def box_of(lanes):
        beta = lax.rem(lanes, 32)
        return 2 * lax.rem(beta, 16) + beta // 16

    def landed(first, count, phase):
        fin[7, first : first + count] = rb[first : first + count, xi]
        arrived(fin.at[pl.ds(0, NX - 1), pl.ds(first, count)], phase)
        size = NX * count * 8
        got = fin[:, first : first + count].astype(F32).reshape(size, 128)
        ident = got[:, 127:128]
        quarter = lax.rem(iota((size, 1), 0), 4).astype(F32)
        key = jnp.where(ident > 0.5, ident - 1.0 + 32.0 * quarter, -1.0)
        landing = one_hot(key.astype(jnp.int32) == iota((size, 128), 1))
        return dot(got.astype(BF16), landing, ((0,), (0,)))

    leaf_sum = landed(0, 12, 6)
    arrived(cpr, 7)
    parent = jnp.concatenate([cpb[...] + cpr[0] + cpr[1] + cpr[2], jnp.zeros((4, M), F32)], axis=0)
    p_box = box_of(iota((8, 128), 1))
    lowered = jnp.zeros((M, 128), F32)
    for o in range(2):
        spread = one_hot((p_box // 8 == row8) & (lax.rem(p_box, 8) == lv * 2 + o))
        octant = dot(parent.astype(BF16), spread, ((0,), (0,))).astype(BF16)
        lowered = lowered + dot(down[o], octant)
    leaf_sum = (leaf_sum + landed(12, 4, 11)).astype(BF16)
    e_box = box_of(lane)
    totals = [dot(leaf_sum[0:CH, :], one_hot(sub == 32 * j + e_box)) for j in range(4)]
    total = jnp.concatenate(totals, axis=0)[0:M, :].astype(BF16)
    fl[...] = dot(cmt[0:M, 0:M], total) + lowered

    def from_surface(i, carry):
        x = [jnp.broadcast_to(xg[c, pl.ds(i, 1), :], (8, 128)) for c in range(3)]
        acc = [jnp.zeros((8, 128), F32) for _ in range(3)]
        for kb in range(K // 8):
            at = kb * 8
            f = [fl[c * K + at : c * K + at + 8, :] for c in range(3)]
            r = [x[c] - shell[c * K + at : c * K + at + 8, :] for c in range(3)]
            q = qst[i, at : at + 8, :]
            wd = wst[i, at : at + 8, :] * (r[0] * f[0] + r[1] * f[1] + r[2] * f[2])
            for c in range(3):
                acc[c] = acc[c] + (q * f[c] + wd * r[c])
        for c in range(3):
            fo[pl.ds(c * 16 + i, 1), :] = jnp.sum(acc[c], axis=0, keepdims=True)
        return carry

    fo[48:128] = jnp.zeros((80, 128), F32)
    lax.fori_loop(0, 16, from_surface, 0)
    back = fo[...].T
    for c in range(3):
        total = jnp.zeros((16, 128), F32)
        for b2 in range(2):
            for g in range(4):
                at = g * 32 + b2 * 16
                pos = b2 * 4 + g
                piece = pltpu.roll(back[at : at + 16, :], (16 * (pos - c)) % 128, 1)
                total = jnp.where(lane16 == pos, piece, total)
        frb[c] = total + nn[c]
    frs[...] = frb[...].astype(BF16)
    for i in range(1, NL):
        send(frs, frr.at[i - 1], 8, (me, y_peer(i)))
    arrived(frr, 8)
    forces = frb[...] + frr[0].astype(F32) + frr[1].astype(F32) + frr[2].astype(F32)
    for c in range(3):
        for m in range(16):
            out_ref[c : c + 1, m * 128 : (m + 1) * 128] = forces[c, m : m + 1, :]

    gone(ppb.at[pl.ds(0, NL - 1)], 0)
    gone(ids.at[pl.ds(0, NL - 1)], 1)
    gone(gz.at[pl.ds(0, 8)], 2)
    gone(gz.at[pl.ds(0, 7)], 12)
    gone(rb.at[pl.ds(0, 6)], 3)
    gone(rb.at[pl.ds(0, 6)], 9)
    gone(rb.at[pl.ds(0, 3)], 10)
    gone(pall.at[pl.ds(0, NX - 1)], 4)
    gone(spb.at[pl.ds(0, NL - 1)], 5)
    gone(fin.at[pl.ds(0, NX - 1), pl.ds(0, 12)], 6)
    gone(fin.at[pl.ds(0, NX - 1), pl.ds(0, 4)], 11)
    gone(cpr, 7)
    gone(frr, 8)


def local_part(
    offsets, vel_cot, m2l_ops, child_ops, check_map, leaf_dest, leaf_slot, coarse_dest,
    coarse_slot, near_box, near_dir,
):
    shell = jnp.asarray(np.repeat(surface_points().reshape(M, 1), 128, axis=1))
    vmem = pl.BlockSpec(memory_space=pltpu.VMEM)
    hbm = pl.BlockSpec(memory_space=pl.ANY)
    V = pltpu.VMEM
    return pl.pallas_call(
        kernel,
        out_shape=jax.ShapeDtypeStruct((3, 2048), F32),
        in_specs=[hbm] * 12,
        out_specs=vmem,
        scratch_shapes=[
            V((3, 2048), F32), V((3, 2048), F32), V((M, 128), F32), V((4, 1, 32), I32),
            V((4, 32), I32), V((4, 1, 512), I32), V((4, 512), I32), pltpu.SMEM((4, 32), I32),
            pltpu.SMEM((4, 32), I32),
            V((4, M, M), BF16), V((2, M, M), BF16), V((M, M), F32), V((512, 512), BF16),
            V((2, M, M), BF16),
            V((8, 2048), F32), V((128, 128), F32), V((128, 128), F32), V((384, 128), BF16), V((32, 8, 128), F32),
            V((6, 16, 128), F32), V((16, K, 128), F32), V((16, K, 128), F32), V((M, 128), F32),
            V((4, 8, 128), F32), V((3, 8, 128), F32), V((4, 8, 512), F32),
            V((NZ, 4, 128), BF16), V((NX, NZ, 4, 128), BF16), V((4, 16, 128), BF16),
            V((4, 16, 128), BF16), V((4, M), F32), V((3, 4, M), F32), V((8, 128), F32), V((128, 512), F32),
            V((NZ, NX, 8, 128), BF16), V((NZ, NX, 8, 128), BF16), V((NX, NZ, 8, 128), BF16),
            V((512, 512), F32), V((M, 128), F32), V((3, 16, 128), F32), V((128, 128), F32),
            V((3, 16, 128), F32), V((3, 16, 128), BF16), V((3, 3, 16, 128), BF16),
            pltpu.SemaphoreType.DMA((12,)), pltpu.SemaphoreType.DMA((13,)),
            pltpu.SemaphoreType.DMA((13,)),
        ],
        compiler_params=pltpu.CompilerParams(collective_id=0, has_side_effects=True),
    )(
        offsets, vel_cot, shell, leaf_dest[0].transpose(1, 2, 0), leaf_slot[0].T,
        coarse_dest[0].transpose(1, 2, 0), coarse_slot[0].T, near_box.T, near_dir.T, child_ops,
        m2l_ops, check_map,
    )


def solution(mesh):
    return jax.shard_map(
        local_part,
        mesh=mesh,
        in_specs=(
            P(None, "leaf"), P(None, "leaf"), P("lvl", None, None), P("lvl", None, None), P(),
            P("lvl", "leaf", None, None), P("lvl", "leaf", None), P("lvl", None, None, None),
            P("lvl", None, None), P("leaf", "lvl"), P("leaf", "lvl"),
        ),
        out_specs=P(None, "leaf"),
        check_vma=False,
    )
```

time: 67.1 us -> 46.6 us (0.69)
  Pallas kernels: 59.8 us -> 44.8 us
  local copies, waits for them, and re-layouts: 5.1 us -> 1.38 us
  other arithmetic: 1.39 us -> 0 us
    pallas_call x1, Pallas kernels: 59.8 us -> 44.8 us  [local_part(): pl.pallas_call(kernel, out_shape=jax.ShapeDtypeStruct((3, 2048), F32), in...]
    unnamed x12 -> x1, local copies, waits for them, and re-layouts: 2.8 us -> 1.38 us
    squeeze x1 -> x0, local copies, waits for them, and re-layouts: 0.96 us -> none  [local_part(): ids = (coarse_dest[0, :, :, 0] * 4 + coarse_slot[0]).reshape(NZ, NX, 4, 4)]
    reshape x1 -> x0, local copies, waits for them, and re-layouts: 0.89 us -> none  [local_part(): jnp.pad(ids, ((0, 4), (0, 0), (0, 0), (0, 4)), constant_values=-1)]
    mul x1 -> x0, other arithmetic: 0.77 us -> none  [local_part(): ids = (coarse_dest[0, :, :, 0] * 4 + coarse_slot[0]).reshape(NZ, NX, 4, 4)]
where the time goes in v2:
time: 46.6 us; the launch traced here: 46.2 us
  Pallas kernels  44.8 us (96%)
  local copies, waits for them, and re-layouts  1.38 us (3%)
    pallas_call x1, Pallas kernels, local_part(): pl.pallas_call(kernel, out_shape=jax.ShapeDtypeStruct((3, 2048), F32), in...  44.8 us
    unnamed x1, local copies, waits for them, and re-layouts  1.38 us

profile of v2, /device:TPU:1, one launch (start us, length us, event | category | flops | bytes accessed | tf_op | source)
XLA Modules:
  0.0 46.2 jit_solution(2062130470676499334)
XLA Ops:
  0.0 44.8 %shard_map.118 = f32[3,2048]{1,0:T(4,128)} custom-call(f32[3,2048]{1,0:T(4,128)} %off_h.1, f32[3,2048]{1,0:T(4,128)} %vel_h.1, f32[456,128]{1,0:T(8,128)} %constant.2.clone.shell_h, s32[4,1,32]{2,1,0:T(1,128)} %bitcast.18, s32[4,32]{1,0:T(4,128)} %bitcast.19, s32[4,1,512]{2,1,0:T(1,128)} %bitcast.16, s32[4,512]{1,0:T(4,128)} %bitcast.17, s32[4,32]{1,0:T(4,128)} %bitcast.20, ...), custom_call_target="tpu_custom_call" | custom-call | tf_op jit(solution)/shard_map/pallas_call | solution.py:441
  44.8 1.4 %copy.15 = f32[3,2048]{1,0:T(4,128)} copy(f32[3,2048]{1,0:T(4,128)} %shard_map.118) | data formatting | bytes 49152

commit v3 on v2

--- a/solution.py
+++ b/solution.py
@@ -13,7 +13,7 @@
 K = 152
 NZ, NX, NL = 16, 8, 4
 CH = 120
-NEAREST = 2
+NEAREST = 4
 F32, BF16, I32 = jnp.float32, jnp.bfloat16, jnp.int32
 MESH = pl.DeviceIdType.MESH
 
@@ -39,7 +39,7 @@
 
 def kernel(
     off_h, vel_h, shell_h, leaf_dest_h, leaf_slot_h, coarse_dest_h, coarse_slot_h, near_box_h,
-    near_dir_h, child_h, m2l_h, cm_h, out_ref,
+    near_dir_h, child_h, m2l_h, cm_h, own_ref, others_ref,
     off, vel, shell, leaf_dest, leaf_slot, coarse_dest, coarse_slot, near_box, near_dir,
     m2l, child, cm, cmt, down, x6, nat, tn, thirds, tab, xg, wst, qst, av, ppb, prs, ids, gz, pall, spb, spr,
     cpb, cpr, meta, tms, sb, rb, fin, wt, fl, nn, fo, frb, frs, frr,
@@ -70,10 +70,6 @@
     def greet_y(k, c):
         pl.semaphore_signal(barrier, 1, device_id=(me, y_peer(k)), device_id_type=MESH)
         return c
-
-    lax.fori_loop(1, NZ, greet_z, 0)
-    lax.fori_loop(1, NX, greet_x, 0)
-    lax.fori_loop(1, NL, greet_y, 0)
 
     loads = [
         pltpu.make_async_copy(src, dst, loc.at[n])
@@ -86,8 +82,13 @@
             )
         )
     ]
-    for load in loads:
+    for load in loads[0:3]:
         load.start()
+    lax.fori_loop(1, NZ, greet_z, 0)
+    lax.fori_loop(1, NX, greet_x, 0)
+    lax.fori_loop(1, NL, greet_y, 0)
+    for n in (9, 3, 4, 5, 6, 10, 7, 8, 11):
+        loads[n].start()
 
     def send(src, dst, phase, device):
         pltpu.make_async_remote_copy(
@@ -101,15 +102,15 @@
     def gone(ref, phase):
         pltpu.make_async_copy(ref, ref, ss.at[phase]).wait()
 
-    groups = ((0, 6), (6, 6), (12, 4))
+    groups = ((0, 8), (8, 4), (12, 4))
 
     def group_of(slot):
-        return 3 if slot < 6 else 9 if slot < 12 else 10
+        return 3 if slot < 8 else 9 if slot < 12 else 10
 
     def forward(g):
         first, count = groups[g]
         arrived(rb.at[pl.ds(first, count - (g == 2))], group_of(first))
-        for i in range(1, NX):
+        for i in (4, 3, 5, 2, 6, 1, 7):
             src, dst = rb.at[pl.ds(first, count), x_peer(i)], fin.at[i - 1, pl.ds(first, count)]
             send(src, dst, 11 if g == 2 else 6, (zi * NX + x_peer(i), lv))
 
@@ -170,7 +171,8 @@
     a = a + pltpu.roll(a, 32, 1)
     b_row, b_lane = iota((32, 128), 0), iota((32, 128), 1)
     pick = one_hot(b_lane == lax.rem(b_row, 2) * 16 + b_row // 2)
-    local = dot(pick, a.astype(BF16), ((1,), (1,))).astype(BF16)
+    summed = a.astype(BF16)
+    local = dot(pick, summed, ((1,), (1,))).astype(BF16)
 
     for load in loads[3:7]:
         load.wait()
@@ -182,21 +184,19 @@
         meta[c : c + 1, 0:32] = leaf_dest[c].astype(F32)
     meta[4:8, 0:32] = leaf_slot[...].astype(F32)
 
-    p_row, c_col = iota((8, 32), 0), iota((8, 32), 1)
+    p_row, p_lane = iota((8, 128), 0), iota((8, 128), 1)
     loads[9].wait()
     part = jnp.zeros((8, M), F32)
     for o in range(2):
-        rows = one_hot((c_col == p_row * 8 + lv * 2 + o) & (p_row < 4))
-        part = part + dot(dot(rows, local).astype(BF16), child[o])
-    ppb[3] = jnp.zeros((8, 128), F32)
+        rows = one_hot((p_lane == o * 16 + p_row * 4 + lv) & (p_row < 4))
+        part = part + dot(dot(rows, summed, ((1,), (1,))).astype(BF16), child[o])
+    ppb[3] = jnp.zeros((4, 128), F32)
     for k in range(3):
-        ppb[k] = part[:, k * 128 : (k + 1) * 128]
-    ppb[3, :, 0 : M - 384] = part[:, 384:M]
+        ppb[k] = part[0:4, k * 128 : (k + 1) * 128]
+    ppb[3, :, 0 : M - 384] = part[0:4, 384:M]
     pl.semaphore_wait(barrier, NZ + NX + NL - 3)
     for i in range(1, NL):
         send(ppb.at[y_peer(i)], prs.at[i - 1], 0, (me, y_peer(i)))
-    for i in range(1, NL):
-        send(ids.at[lv], ids.at[lv], 1, (me, y_peer(i)))
 
     loads[10].wait()
     tms[:, 384:512] = jnp.zeros((128, 128), F32)
@@ -236,11 +236,13 @@
 
     arrived(prs, 0)
     mine = ppb[lv] + prs[0] + prs[1] + prs[2]
-    gz[4] = mine[0:4].astype(BF16)
+    gz[4] = mine.astype(BF16)
     for k in (8, 7, 9, 6, 10, 5, 11, 4, 12, 3, 13, 2, 14, 1, 15):
         slot = (4 - k) % NZ
         send(gz.at[4], gz.at[slot], 2 if slot < 9 else 12, (z_peer(k) * NX + xi, lv))
     leaf_z(NEAREST, 15)
+    for i in range(1, NL):
+        send(ids.at[lv], ids.at[lv], 1, (me, y_peer(i)))
 
     row8 = iota((8, 128), 0)
     loads[7].wait()
@@ -300,7 +302,7 @@
 
     for first, count, phase in ((0, 9, 2), (9, 7, 12)):
         arrived(gz.at[pl.ds(first, min(count, 8))], phase)
-        for i in range(1, NX):
+        for i in (4, 3, 5, 2, 6, 1, 7):
             part = gz.at[pl.ds(first, count)]
             send(part, pall.at[xi, pl.ds(first, count)], 4, (zi * NX + x_peer(i), lv))
     pall[xi] = gz[...]
@@ -409,18 +411,22 @@
     frs[...] = frb[...].astype(BF16)
     for i in range(1, NL):
         send(frs, frr.at[i - 1], 8, (me, y_peer(i)))
+
+    def spread_out(ref, forces):
+        for c in range(3):
+            for m in range(16):
+                ref[c : c + 1, m * 128 : (m + 1) * 128] = forces[c, m : m + 1, :]
+
+    spread_out(own_ref, frb[...])
     arrived(frr, 8)
-    forces = frb[...] + frr[0].astype(F32) + frr[1].astype(F32) + frr[2].astype(F32)
-    for c in range(3):
-        for m in range(16):
-            out_ref[c : c + 1, m * 128 : (m + 1) * 128] = forces[c, m : m + 1, :]
+    spread_out(others_ref, frr[0].astype(F32) + frr[1].astype(F32) + frr[2].astype(F32))
 
     gone(ppb.at[pl.ds(0, NL - 1)], 0)
     gone(ids.at[pl.ds(0, NL - 1)], 1)
     gone(gz.at[pl.ds(0, 8)], 2)
     gone(gz.at[pl.ds(0, 7)], 12)
-    gone(rb.at[pl.ds(0, 6)], 3)
-    gone(rb.at[pl.ds(0, 6)], 9)
+    gone(rb.at[pl.ds(0, 8)], 3)
+    gone(rb.at[pl.ds(0, 4)], 9)
     gone(rb.at[pl.ds(0, 3)], 10)
     gone(pall.at[pl.ds(0, NX - 1)], 4)
     gone(spb.at[pl.ds(0, NL - 1)], 5)
@@ -438,11 +444,11 @@
     vmem = pl.BlockSpec(memory_space=pltpu.VMEM)
     hbm = pl.BlockSpec(memory_space=pl.ANY)
     V = pltpu.VMEM
-    return pl.pallas_call(
+    own, others = pl.pallas_call(
         kernel,
-        out_shape=jax.ShapeDtypeStruct((3, 2048), F32),
+        out_shape=[jax.ShapeDtypeStruct((3, 2048), F32)] * 2,
         in_specs=[hbm] * 12,
-        out_specs=vmem,
+        out_specs=[vmem] * 2,
         scratch_shapes=[
             V((3, 2048), F32), V((3, 2048), F32), V((M, 128), F32), V((4, 1, 32), I32),
             V((4, 32), I32), V((4, 1, 512), I32), V((4, 512), I32), pltpu.SMEM((4, 32), I32),
@@ -451,7 +457,7 @@
             V((2, M, M), BF16),
             V((8, 2048), F32), V((128, 128), F32), V((128, 128), F32), V((384, 128), BF16), V((32, 8, 128), F32),
             V((6, 16, 128), F32), V((16, K, 128), F32), V((16, K, 128), F32), V((M, 128), F32),
-            V((4, 8, 128), F32), V((3, 8, 128), F32), V((4, 8, 512), F32),
+            V((4, 4, 128), F32), V((3, 4, 128), F32), V((4, 8, 512), F32),
             V((NZ, 4, 128), BF16), V((NX, NZ, 4, 128), BF16), V((4, 16, 128), BF16),
             V((4, 16, 128), BF16), V((4, M), F32), V((3, 4, M), F32), V((8, 128), F32), V((128, 512), F32),
             V((NZ, NX, 8, 128), BF16), V((NZ, NX, 8, 128), BF16), V((NX, NZ, 8, 128), BF16),
@@ -466,6 +472,7 @@
         coarse_dest[0].transpose(1, 2, 0), coarse_slot[0].T, near_box.T, near_dir.T, child_ops,
         m2l_ops, check_map,
     )
+    return own + others
 
 
 def solution(mesh):

time: 46.6 us -> 46.3 us (level)
  other arithmetic: 0 us -> 1.4 us
  local copies, waits for them, and re-layouts: 1.38 us -> 0 us
    add x0 -> x1, other arithmetic: none -> 1.4 us  [local_part(): return own + others]
    unnamed x1 -> x0, local copies, waits for them, and re-layouts: 1.38 us -> none
where the time goes in v3:
time: 46.3 us; the launch traced here: 46.2 us
  Pallas kernels  44.7 us (97%)
  other arithmetic  1.4 us (3%)
    pallas_call x1, Pallas kernels, local_part(): pl.pallas_call(kernel, out_shape=[jax.ShapeDtypeStruct((3, 2048), F32)] *...  44.7 us
    add x1, other arithmetic, local_part(): return own + others  1.4 us

profile of v3, /device:TPU:1, one launch (start us, length us, event | category | flops | bytes accessed | tf_op | source)
XLA Modules:
  0.0 46.2 jit_solution(1458823746549578655)
XLA Ops:
  0.0 44.7 %shard_map.118 = (f32[3,2048]{1,0:T(4,128)}, f32[3,2048]{1,0:T(4,128)}) custom-call(f32[3,2048]{1,0:T(4,128)} %off_h.1, f32[3,2048]{1,0:T(4,128)} %vel_h.1, f32[456,128]{1,0:T(8,128)} %constant.2.clone.shell_h, s32[4,1,32]{2,1,0:T(1,128)} %bitcast.18, s32[4,32]{1,0:T(4,128)} %bitcast.19, s32[4,1,512]{2,1,0:T(1,128)} %bitcast.16, s32[4,512]{1,0:T(4,128)} %bitcast.17, ...), custom_call_target="tpu_custom_call" | custom-call | tf_op jit(solution)/shard_map/pallas_call | solution.py:447
  44.8 1.4 %add.3 = f32[3,2048]{1,0:T(4,128)} add(f32[3,2048]{1,0:T(4,128)} %get-tuple-element.7, f32[3,2048]{1,0:T(4,128)} %get-tuple-element.8) | non-fusion elementwise | flops 6144 | bytes 73728 | tf_op jit(solution)/shard_map/add | solution.py:475

commit v4 on v3

--- a/solution.py
+++ b/solution.py
@@ -84,7 +84,8 @@
     ]
     for load in loads[0:3]:
         load.start()
-    lax.fori_loop(1, NZ, greet_z, 0)
+    for k in (8, 7, 9, 6, 10, 5, 11, 4, 12, 3, 13, 2, 14, 1, 15):
+        greet_z(k, 0)
     lax.fori_loop(1, NX, greet_x, 0)
     lax.fori_loop(1, NL, greet_y, 0)
     for n in (9, 3, 4, 5, 6, 10, 7, 8, 11):
@@ -397,7 +398,7 @@
         return carry
 
     fo[48:128] = jnp.zeros((80, 128), F32)
-    lax.fori_loop(0, 16, from_surface, 0)
+    lax.fori_loop(0, 16, from_surface, 0, unroll=4)
     back = fo[...].T
     for c in range(3):
         total = jnp.zeros((16, 128), F32)

time: 46.3 us -> 46.1 us (level)
  no operation moved by 1% of the time
where the time goes in v4:
time: 46.1 us; the launch traced here: 45.9 us
  Pallas kernels  44.5 us (97%)
  other arithmetic  1.4 us (3%)
    pallas_call x1, Pallas kernels, local_part(): pl.pallas_call(kernel, out_shape=[jax.ShapeDtypeStruct((3, 2048), F32)] *...  44.5 us
    add x1, other arithmetic, local_part(): return own + others  1.4 us

profile of v4, /device:TPU:1, one launch (start us, length us, event | category | flops | bytes accessed | tf_op | source)
XLA Modules:
  0.0 45.9 jit_solution(9054145086766237817)
XLA Ops:
  0.0 44.5 %shard_map.118 = (f32[3,2048]{1,0:T(4,128)}, f32[3,2048]{1,0:T(4,128)}) custom-call(f32[3,2048]{1,0:T(4,128)} %off_h.1, f32[3,2048]{1,0:T(4,128)} %vel_h.1, f32[456,128]{1,0:T(8,128)} %constant.2.clone.shell_h, s32[4,1,32]{2,1,0:T(1,128)} %bitcast.18, s32[4,32]{1,0:T(4,128)} %bitcast.19, s32[4,1,512]{2,1,0:T(1,128)} %bitcast.16, s32[4,512]{1,0:T(4,128)} %bitcast.17, ...), custom_call_target="tpu_custom_call" | custom-call | tf_op jit(solution)/shard_map/pallas_call | solution.py:448
  44.5 1.4 %add.3 = f32[3,2048]{1,0:T(4,128)} add(f32[3,2048]{1,0:T(4,128)} %get-tuple-element.7, f32[3,2048]{1,0:T(4,128)} %get-tuple-element.8) | non-fusion elementwise | flops 6144 | bytes 73728 | tf_op jit(solution)/shard_map/add | solution.py:476
